TPU v7x, 32 devices: a whole 2x2x4 slice. The times are simulated.
32 devices in a mesh: grid: 32 (over z, y, x, core).
Axes of the slice: x: 2, y: 2, z: 4, core: 2. Of those that a mesh axis runs over, the one named last changes fastest.
Arguments:
- right_sides: float32 [32, 32, 48, 128], P(None, 'grid'), may hold values from -54 to 54, as said below
- recycle: float32 [2, 24, 32, 48, 128], P(None, None, 'grid'), may hold values from -6 to 6
- medium: float32 [32, 48, 128], P('grid'), may hold values from 0.05 to 1
- shift_table: float32 [8], replicated, may hold values from 0.25 to 2
- shift_index: int32 [2], replicated, may hold values from 0 to 7
Outputs:
- solution: float32 [32, 32, 48, 128], P(None, 'grid')
- residue: float32 [32, 32, 48, 128], P(None, 'grid')
Inputs may be any that keep to these rules, and one draw needn't show every extreme that they name: `right_sides`: finite real values.
All inputs are finite; a program needn't handle non-finite values.
Results may differ from a plain program's by a relative error of at most 0.0003.
Values sent between devices are 32-bit elements; how exact they have to be, the bound alone decides.
A program may use at most 64 MiB of HBM per device.

v0:
```python
import functools

import jax
import jax.numpy as jnp
from jax import lax
from jax.experimental import pallas as pl
from jax.experimental.pallas import tpu as pltpu
from jax.sharding import PartitionSpec as P

STEPS = 3
LANES = 128
MESH = pl.DeviceIdType.MESH
highest = lax.Precision.HIGHEST


def dot(left, right):
    return lax.dot_general(
        left, right, (((1,), (0,)), ((), ())), precision=highest, preferred_element_type=jnp.float32
    )


def dot_t(left, right):
    return lax.dot_general(
        left, right, (((1,), (1,)), ((), ())), precision=highest, preferred_element_type=jnp.float32
    )


def halves(x):
    high = x.astype(jnp.bfloat16)
    return high, (x - high.astype(jnp.float32)).astype(jnp.bfloat16)


def dot_three(left, right):
    a, b = halves(left), halves(right)
    one = lambda p, q: jnp.dot(p, q, preferred_element_type=jnp.float32)
    return one(a[0], b[0]) + (one(a[0], b[1]) + one(a[1], b[0]))


def iota2(shape, dim):
    return lax.broadcasted_iota(jnp.int32, shape, dim)


def eye(size):
    return jnp.where(iota2((size, size), 0) == iota2((size, size), 1), 1.0, 0.0)


def pair_step(arrays, k, first, second):
    c1, c2 = arrays[0][:, k : k + 1], arrays[0][:, k + 1 : k + 2]
    f1 = jnp.where(first, c1 * (1.0 / c1[k : k + 1]), 0.0)
    c2 = c2 - f1 * c2[k : k + 1]
    f2 = jnp.where(second, c2 * (1.0 / c2[k + 1 : k + 2]), 0.0)
    link = f1[k + 1 : k + 2]
    out = []
    for x in arrays:
        r1 = x[k : k + 1, :]
        r2 = x[k + 1 : k + 2, :] - link * r1
        out.append(x - f1 * r1 - f2 * r2)
    return tuple(out)


def factor_all(matrices, count):
    size = matrices[0].shape[0]
    rows = iota2((size, 1), 0)
    unit = jnp.where(rows < count, eye(size), 0.0)
    parts = [(m, unit) for m in matrices]
    for k in range(0, count, 2):
        parts = [pair_step(p, k, rows > k, rows > k + 1) for p in parts]
    upper = iota2((size, size), 1) >= iota2((size, size), 0)
    out = []
    for a, z in parts:
        pivots = jnp.sum(a * unit, axis=1, keepdims=True)
        root = jnp.where(rows < count, lax.rsqrt(jnp.where(rows < count, pivots, 1.0)), 0.0)
        out.append((jnp.where(upper, a * root, 0.0), z * root))
    return out


def solve_all(matrices, rights):
    size = matrices[0].shape[0]
    rows = iota2((size, 1), 0)
    unit = eye(size)
    parts = list(zip(matrices, rights))
    for k in range(0, size, 2):
        parts = [pair_step(p, k, rows != k, rows != k + 1) for p in parts]
    return [r / jnp.sum(a * unit, axis=1, keepdims=True) for a, r in parts]


def kernel(
    n, factors, chunk,
    u_ref, b_ref, med_ref, table_ref, index_ref, sol_ref, res_ref,
    space, halo_u, halo_v, gram0, gram, coef, hbt, ebt, fin, back,
    send_sem, recv_sem, red_send, red_recv,
):
    me = lax.axis_index("grid")
    k_rows = u_ref.shape[1]
    block = b_ref.shape[1]
    cells = b_ref.shape[2]
    count = cells // chunk
    pad = space.shape[1] - (STEPS + 1) * block
    left, right = me - 1, me + 1
    has = (me > 0, me < n - 1)

    barrier = pltpu.get_barrier_semaphore()
    peers = []
    stride = 1
    for f in factors:
        mine = lax.rem(me // stride, f)
        base = me - mine * stride
        peers.append((f, stride, mine, base))
        stride *= f
    total = 0
    for f, stride, mine, base in peers:
        for d in range(1, f):
            pl.semaphore_signal(
                barrier, inc=1, device_id=(base + lax.rem(mine + d, f) * stride,), device_id_type=MESH
            )
            total += 1
    for to in (lax.rem(me + n - 1, n), lax.rem(me + 1, n)):
        pl.semaphore_signal(barrier, inc=1, device_id=(to,), device_id_type=MESH)
    pl.semaphore_wait(barrier, total + 2)

    def halo_copy(stage, side, i):
        inner = pl.ds(pl.multiple_of(i * chunk, LANES), chunk)
        outer = pl.ds(pl.multiple_of(i * chunk + LANES, LANES), chunk)
        if stage == 0:
            src, dst = u_ref.at[:, :, outer], halo_u.at[side, :, :, inner]
        else:
            src = space.at[:, pl.ds(pad + block * (stage - 1), block), outer]
            dst = halo_v.at[stage - 1, side, :, :, inner]
        return pltpu.make_async_remote_copy(
            src_ref=src, dst_ref=dst,
            send_sem=send_sem.at[stage, side, i], recv_sem=recv_sem.at[stage, side, i],
            device_id=((left, right)[side],), device_id_type=MESH,
        )

    def halo_start(stage, i):
        for side in range(2):
            @pl.when(has[side])
            def _():
                halo_copy(stage, side, i).start()

    def halo_wait(stage, i):
        for side in range(2):
            @pl.when(has[1 - side])
            def _():
                halo_copy(stage, side, i).wait_recv()

    def reduce_sum(buffer, number, values):
        offset = 0
        for f, stride, mine, base in peers:
            own = offset + mine
            for g in range(len(values)):
                buffer[number, own, g, :, :] = values[g]
            for d in range(1, f):
                to = lax.rem(mine + d, f)
                pltpu.make_async_remote_copy(
                    src_ref=buffer.at[number, own], dst_ref=buffer.at[number, own],
                    send_sem=red_send.at[number if buffer is gram0 else number + 1, offset + d],
                    recv_sem=red_recv.at[number if buffer is gram0 else number + 1, own],
                    device_id=(base + to * stride,), device_id_type=MESH,
                ).start()
            for d in range(1, f):
                there = lax.rem(mine + d, f)
                origin = offset + there
                pltpu.make_async_remote_copy(
                    src_ref=buffer.at[number, origin], dst_ref=buffer.at[number, origin],
                    send_sem=red_send.at[number if buffer is gram0 else number + 1, offset + d],
                    recv_sem=red_recv.at[number if buffer is gram0 else number + 1, origin],
                    device_id=(base + there * stride,), device_id_type=MESH,
                ).wait_recv()
            held = len(values)
            values = []
            for g in range(held):
                value = buffer[number, offset, g, :, :]
                for s in range(1, f):
                    value = value + buffer[number, offset + s, g, :, :]
                values.append(value)
            offset += f
        return values

    def reduce_drain(buffer, number):
        offset = 0
        for f, stride, mine, base in peers:
            for d in range(1, f):
                pltpu.make_async_remote_copy(
                    src_ref=buffer.at[number, offset + mine], dst_ref=buffer.at[number, offset + mine],
                    send_sem=red_send.at[number if buffer is gram0 else number + 1, offset + d],
                    recv_sem=red_recv.at[number if buffer is gram0 else number + 1, offset + mine],
                    device_id=(base + lax.rem(mine + d, f) * stride,), device_id_type=MESH,
                ).wait_send()
            offset += f

    def send_loop(i, carry):
        halo_start(0, i)
        return carry

    lax.fori_loop(0, count, send_loop, 0)

    shifts = []
    for g in range(2):
        shift = jnp.float32(0.0)
        for s in range(table_ref.shape[0]):
            shift = shift + jnp.where(index_ref[g] == s, table_ref[s], 0.0)
        shifts.append(6.0 + shift)

    zero_rows = space.shape[1]
    for g in range(2):
        space[g, :, 0:LANES] = jnp.zeros((zero_rows, LANES), jnp.float32)
        space[g, :, cells + LANES : cells + 2 * LANES] = jnp.zeros((zero_rows, LANES), jnp.float32)
        if pad > k_rows:
            space[g, k_rows:pad, :] = jnp.zeros((pad - k_rows, space.shape[2]), jnp.float32)
    for side in range(2):
        @pl.when(jnp.logical_not(has[1 - side]))
        def _():
            halo_u[side] = jnp.zeros(halo_u.shape[1:], jnp.float32)
            for j in range(STEPS):
                halo_v[j, side] = jnp.zeros(halo_v.shape[2:], jnp.float32)

    lane = iota2((1, LANES), 1)

    def stencil(load, side0, side1, g, start):
        outer = start + LANES
        c = load(outer)
        near = load(outer - LANES) + load(outer + LANES)
        near = near + side0 + side1
        near = near + jnp.where(lane == 0, 0.0, pltpu.roll(c, 1, 1))
        near = near + jnp.where(lane == LANES - 1, 0.0, pltpu.roll(c, LANES - 1, 1))
        diag = med_ref[:, pl.ds(start, LANES)] + shifts[g]
        return diag * c - near

    def first_chunk(i, carry):
        halo_wait(0, i)
        out = []
        for g in range(2):
            for q in range(chunk // LANES):
                start = pl.multiple_of(i * chunk + q * LANES, LANES)
                here = pl.ds(start, LANES)
                applied = stencil(
                    lambda at: u_ref[g, :, pl.ds(pl.multiple_of(at, LANES), LANES)],
                    halo_u[0, g, :, here], halo_u[1, g, :, here], g, start,
                )
                there = pl.ds(pl.multiple_of(start + LANES, LANES), LANES)
                space[g, 0:k_rows, there] = applied
                space[g, pad : pad + block, there] = b_ref[g, :, here]
            outer = pl.ds(pl.multiple_of(i * chunk + LANES, LANES), chunk)
            rows = space[g, 0 : pad + block, outer]
            out.append(carry[g] + dot_t(rows, rows))
        return tuple(out)

    size = pad + block
    zero = jnp.zeros((size, size), jnp.float32)
    sums = lax.fori_loop(0, count, first_chunk, (zero, zero))
    half = LANES // 2
    fin[0, 0:size, :] = jnp.zeros((size, LANES), jnp.float32)
    for g in range(2):
        fin[0, 0:size, half * g : half * g + size] = sums[g]
    fin[0, 0:size, :] = reduce_sum(gram0, 0, [fin[0, 0:size, :]])[0]
    fin[1, 0:size, 0:size] = fin[0, 0:size, half : half + size]
    linv = [z for _, z in factor_all([fin[g, 0:pad, 0:pad] for g in range(2)], k_rows)]
    proj_t = [dot_t(fin[g, pad:size, 0:pad], linv[g]) for g in range(2)]
    remaining = [fin[g, pad:size, pad:size] - dot_t(proj_t[g], proj_t[g]) for g in range(2)]
    first_factor = factor_all(remaining, block)
    for g in range(2):
        inv = first_factor[g][1]
        coef[g, :, 0:pad] = -dot(inv, dot(proj_t[g], linv[g]))
        coef[g, :, pad:size] = inv
        hbt[g, :, :] = jnp.zeros(hbt.shape[1:], jnp.float32)

    unit = eye(block)
    for j in range(1, STEPS + 1):
        known = pad + block * j

        def combine_chunk(i, carry):
            outer = pl.ds(pl.multiple_of(i * chunk + LANES, LANES), chunk)
            for g in range(2):
                space[g, known - block : known, outer] = dot(
                    coef[g, :, 0:known], space[g, 0:known, outer]
                )
            halo_start(j, i)
            return carry

        lax.fori_loop(0, count, combine_chunk, 0)

        def gram_chunk(i, carry):
            halo_wait(j, i)
            out = []
            for g in range(2):
                for q in range(chunk // LANES):
                    start = pl.multiple_of(i * chunk + q * LANES, LANES)
                    here = pl.ds(start, LANES)
                    space[g, known : known + block, pl.ds(pl.multiple_of(start + LANES, LANES), LANES)] = stencil(
                        lambda at: space[g, known - block : known, pl.ds(pl.multiple_of(at, LANES), LANES)],
                        halo_v[j - 1, 0, g, :, here], halo_v[j - 1, 1, g, :, here], g, start,
                    )
                outer = pl.ds(pl.multiple_of(i * chunk + LANES, LANES), chunk)
                rows = space[g, 0 : known + block, outer]
                out.append(carry[g] + dot_t(rows[known:, :], rows))
            return tuple(out)

        zero = jnp.zeros((block, known + block), jnp.float32)
        sums = lax.fori_loop(0, count, gram_chunk, (zero, zero))
        for g in range(2):
            fin[g, 0:block, 0 : known + block] = sums[g]
        sums = reduce_sum(gram, j - 1, [fin[g, 0:block, :] for g in range(2)])
        for g in range(2):
            fin[g, 0:block, :] = sums[g]
        et = [dot_t(fin[g, 0:block, 0:pad], linv[g]) for g in range(2)]
        ht = [fin[g, 0:block, pad:known] for g in range(2)]
        fresh = [
            fin[g, 0:block, known : known + block] - dot_t(et[g], et[g]) - dot_t(ht[g], ht[g])
            for g in range(2)
        ]
        parts = factor_all(fresh, block)
        for g in range(2):
            lt, inv = parts[g]
            coef[g, :, 0:pad] = -dot(inv, dot(et[g], linv[g]))
            coef[g, :, pad:known] = -dot(inv, ht[g])
            coef[g, :, known : known + block] = inv
            at = block * (j - 1)
            hbt[g, at : at + block, 0 : known - pad] = ht[g]
            hbt[g, at : at + block, known - pad : known - pad + block] = dot_t(unit, lt)
            ebt[g, at : at + block, :] = et[g]

    width = pad + block * (STEPS + 1)
    kry = block * STEPS
    normal, rights = [], []
    for g in range(2):
        h = hbt[g, :, 0 : kry + block]
        normal.append(dot_t(h, h))
        rights.append(dot(hbt[g, :, 0:block], first_factor[g][0]))
    ys = solve_all(normal, rights)
    for g in range(2):
        yt = dot_t(unit, ys[g])
        back[g, :, :] = dot(proj_t[g] - dot(yt, ebt[g, :, :]), linv[g])
        rest = -dot(yt, hbt[g, :, :])
        fin[g, 0:block, :] = rest
        fin[g, 0:block, 0:block] = fin[g, 0:block, 0:block] + dot_t(unit, first_factor[g][0])
        top = fin[g, 0:block, 0:kry]
        last = dot(fin[g, 0:block, kry : kry + block], coef[g, :, 0:width])
        fin[g, 0 : 2 * block, :] = jnp.zeros((2 * block, LANES), jnp.float32)
        fin[g, 0:block, pad : pad + kry] = yt
        fin[g, block : 2 * block, 0:width] = last
        fin[g, block : 2 * block, pad : pad + kry] = fin[g, block : 2 * block, pad : pad + kry] + top

    def final_chunk(i, carry):
        outer = pl.ds(pl.multiple_of(i * chunk + LANES, LANES), chunk)
        inner = pl.ds(pl.multiple_of(i * chunk, LANES), chunk)
        for g in range(2):
            both = dot_three(fin[g, 0 : 2 * block, 0:width], space[g, 0:width, outer])
            sol_ref[g, :, inner] = both[0:block] + dot_three(back[g, :, 0:k_rows], u_ref[g, :, outer])
            res_ref[g, :, inner] = both[block:]
        return carry

    lax.fori_loop(0, count, final_chunk, 0)

    for stage in range(STEPS + 1):
        def drain(i, carry):
            for side in range(2):
                @pl.when(has[side])
                def _():
                    halo_copy(stage, side, i).wait_send()
            return carry

        lax.fori_loop(0, count, drain, 0)
    reduce_drain(gram0, 0)
    for j in range(STEPS):
        reduce_drain(gram, j)


def split_count(n):
    out = []
    while n > 1:
        f = next(f for f in (8, 4, 2, n) if n % f == 0)
        out.append(f)
        n //= f
    return out


def solution(mesh):
    n = mesh.shape["grid"]
    factors = split_count(n)

    def on_device(right_sides, recycle, medium, shift_table, shift_index):
        block = right_sides.shape[0] // 2
        k_rows = recycle.shape[1]
        cells = right_sides.shape[2] * right_sides.shape[3]
        pad = -(-k_rows // block) * block
        tiles = cells // LANES
        chunk = LANES * next(t for t in (6, 4, 3, 2, 1) if tiles % t == 0)
        count = cells // chunk
        width = pad + block * (STEPS + 1)
        b = right_sides.reshape(2, block, cells)
        u = jnp.pad(recycle.reshape(2, k_rows, cells), ((0, 0), (0, 0), (LANES, LANES)))
        slots = sum(factors)
        vmem = pl.BlockSpec(memory_space=pltpu.VMEM)
        smem = pl.BlockSpec(memory_space=pltpu.SMEM)
        shape = jax.ShapeDtypeStruct((2, block, cells), jnp.float32)
        f32 = jnp.float32
        sol, res = pl.pallas_call(
            functools.partial(kernel, n, factors, chunk),
            out_shape=(shape, shape),
            in_specs=[vmem, vmem, vmem, smem, smem],
            out_specs=(vmem, vmem),
            scratch_shapes=[
                pltpu.VMEM((2, width, cells + 2 * LANES), f32),
                pltpu.VMEM((2, 2, k_rows, cells), f32),
                pltpu.VMEM((STEPS, 2, 2, block, cells), f32),
                pltpu.VMEM((1, slots, 1, pad + block, LANES), f32),
                pltpu.VMEM((STEPS, slots, 2, block, LANES), f32),
                pltpu.VMEM((2, block, LANES), f32),
                pltpu.VMEM((2, block * STEPS, LANES), f32),
                pltpu.VMEM((2, block * STEPS, pad), f32),
                pltpu.VMEM((2, pad + block, LANES), f32),
                pltpu.VMEM((2, block, pad), f32),
                pltpu.SemaphoreType.DMA((STEPS + 1, 2, count)),
                pltpu.SemaphoreType.DMA((STEPS + 1, 2, count)),
                pltpu.SemaphoreType.DMA((STEPS + 1, slots)),
                pltpu.SemaphoreType.DMA((STEPS + 1, slots)),
            ],
            compiler_params=pltpu.CompilerParams(
                collective_id=0, has_side_effects=True, vmem_limit_bytes=48 * 1024 * 1024
            ),
        )(u, b, medium.reshape(1, cells), shift_table, shift_index)
        return sol.reshape(right_sides.shape), res.reshape(right_sides.shape)

    rows = P(None, "grid", None, None)
    return jax.shard_map(
        on_device,
        mesh=mesh,
        in_specs=(rows, P(None, None, "grid", None, None), P("grid", None, None), P(), P()),
        out_specs=(rows, rows),
        check_vma=False,
    )
```

profile of v0, /device:TPU:0, one launch (start us, length us, event | category | flops | bytes accessed | tf_op | source)
XLA Modules:
  0.0 154.3 jit_solution(16950569668915188116)
XLA Ops:
  0.6 0.0 copy-start.3
  0.6 1.4 reshape.20.b_ref
  2.0 0.1 copy-done.3
  2.1 0.2 reshape.19
  2.3 0.0 copy-start
  2.3 0.0 copy-start.1
  2.3 0.0 copy-start.2
  2.4 0.1 pad.4.u_ref
  2.4 0.6 copy-done
  3.1 0.0 copy-done.1
  3.1 0.0 copy-done.2
  3.1 149.2 %shard_map.68 = (f32[2,16,6144]{2,1,0:T(8,128)S(1)}, f32[2,16,6144]{2,1,0:T(8,128)S(1)}) custom-call(f32[2,24,6400]{2,1,0:T(8,128)S(1)} %pad.4.u_ref, f32[2,16,6144]{2,1,0:T(8,128)S(1)} %reshape.20.b_ref, f32[1,6144]{1,0:T(1,128)S(1)} %bitcast.21, f32[8]{0:T(128)S(1)} %copy-done.1, s32[2]{0:T(128)S(1)} %copy-done.2), custom_call_target="tpu_custom_call" | custom-call | tf_op jit(solution)/shard_map/pallas_call | solution.py:398
  152.3 1.0 copy.9
  153.3 1.0 copy.10
Async XLA Ops:
  0.6 1.5 copy-start.3
  2.3 0.7 copy-start
  2.3 0.7 copy-start.1
  2.3 0.7 copy-start.2
where the time goes:
time: 155 us; the launch traced here: 154 us
  Pallas kernels  149 us (96%)
  local copies, waits for them, and re-layouts  4.43 us (3%)
    pallas_call x1, Pallas kernels, on_device(): pl.pallas_call(functools.partial(kernel, n, factors, chunk), out_shape=(s...  149 us

commit v1 on v0

v1 whole, which is shorter than its diff:
```python
import functools

import jax
import jax.numpy as jnp
from jax import lax
from jax.experimental import pallas as pl
from jax.experimental.pallas import tpu as pltpu
from jax.sharding import PartitionSpec as P

STEPS = 3
LANES = 128
MESH = pl.DeviceIdType.MESH
highest = lax.Precision.HIGHEST


def dot(left, right):
    return lax.dot_general(
        left, right, (((1,), (0,)), ((), ())), precision=highest, preferred_element_type=jnp.float32
    )


def dot_t(left, right):
    return lax.dot_general(
        left, right, (((1,), (1,)), ((), ())), precision=highest, preferred_element_type=jnp.float32
    )


def halves(x):
    high = x.astype(jnp.bfloat16)
    return high, (x - high.astype(jnp.float32)).astype(jnp.bfloat16)


def thirds(x):
    high, low = halves(x)
    return high, low, (x - high.astype(jnp.float32) - low.astype(jnp.float32)).astype(jnp.bfloat16)


def one(left, right):
    return jnp.dot(left, right, preferred_element_type=jnp.float32)


def one_t(left, right):
    return lax.dot_general(left, right, (((1,), (1,)), ((), ())), preferred_element_type=jnp.float32)


def iota2(shape, dim):
    return lax.broadcasted_iota(jnp.int32, shape, dim)


def eye(size):
    return jnp.where(iota2((size, size), 0) == iota2((size, size), 1), 1.0, 0.0)


def pair_step(arrays, k, first, second):
    c1, c2 = arrays[0][:, k : k + 1], arrays[0][:, k + 1 : k + 2]
    f1 = jnp.where(first, c1 * (1.0 / c1[k : k + 1]), 0.0)
    c2 = c2 - f1 * c2[k : k + 1]
    f2 = jnp.where(second, c2 * (1.0 / c2[k + 1 : k + 2]), 0.0)
    link = f1[k + 1 : k + 2]
    out = []
    for x in arrays:
        r1 = x[k : k + 1, :]
        r2 = x[k + 1 : k + 2, :] - link * r1
        out.append(x - f1 * r1 - f2 * r2)
    return tuple(out)


def factor(matrix, count):
    size = matrix.shape[0]
    rows = iota2((size, 1), 0)
    unit = jnp.where(rows < count, eye(size), 0.0)
    parts = (matrix, unit)
    for k in range(0, count, 2):
        parts = pair_step(parts, k, rows > k, rows > k + 1)
    a, z = parts
    upper = iota2((size, size), 1) >= iota2((size, size), 0)
    pivots = jnp.sum(a * unit, axis=1, keepdims=True)
    root = jnp.where(rows < count, lax.rsqrt(jnp.where(rows < count, pivots, 1.0)), 0.0)
    return jnp.where(upper, a * root, 0.0), z * root


def solve(matrix, right):
    size = matrix.shape[0]
    rows = iota2((size, 1), 0)
    parts = (matrix, right)
    for k in range(0, size, 2):
        parts = pair_step(parts, k, rows != k, rows != k + 1)
    a, r = parts
    return r / jnp.sum(a * eye(size), axis=1, keepdims=True)


def gray(j):
    return j + (j // 2) * (1 - 2 * lax.rem(j, 2))


def flip(t, d, bits):
    out = t
    for b in range(bits):
        out = out + (1 << b) * ((d >> b) & 1) * (1 - 2 * lax.rem(t // (1 << b), 2))
    return out


def kernel(
    n, quarters, stages,
    u_ref, b_ref, med_ref, table_ref, index_ref, sol_ref, res_ref,
    ubuf, vbuf, bbuf, mbuf, sh, sl, uh, ul, obuf, gram0, gram, coef, hbt, ebt, fin, back,
    in_send, in_recv, z_send, z_recv, x_send, x_recv, red_send, red_recv, out_send, out_recv,
):
    me = lax.axis_index("grid")
    planes = 2 * quarters
    bits = planes.bit_length() - 1
    k_rows = u_ref.shape[1]
    block = b_ref.shape[1]
    cells = b_ref.shape[2]
    ci = cells // quarters
    cw = ci + 2 * LANES
    tiles = ci // LANES
    pad = -(-k_rows // block) * block
    layers = n // planes
    lay, t = me // planes, lax.rem(me, planes)
    base = lay * planes
    core, q = lax.rem(t, 2), gray(t // 2)
    has_z = (lay > 0, lay < layers - 1)
    has_x = (q > 0, q < quarters - 1)
    z_to = (me - planes, me + planes)
    x_to = tuple(base + 2 * gray(q + s) + core for s in (-1, 1))

    barrier = pltpu.get_barrier_semaphore()
    peers = []
    for f, stride in stages:
        mine = lax.rem(me // stride, f)
        peers.append((f, stride, mine, me - mine * stride))
    greet = [base + flip(t, d, bits) for d in range(1, planes)]
    for f, stride, mine, first in peers:
        if stride >= planes:
            greet += [first + lax.rem(mine + d, f) * stride for d in range(1, f)]
    if layers > 1:
        greet += [lax.rem(me + planes, n), lax.rem(me + n - planes, n)]
    for to in greet:
        pl.semaphore_signal(barrier, inc=1, device_id=(to,), device_id_type=MESH)
    pl.semaphore_wait(barrier, len(greet))

    def part(qq, width):
        return pl.ds(pl.multiple_of(qq * ci, LANES), width)

    def in_copy(kind, there):
        to_core, to_q = lax.rem(there, 2), gray(there // 2)
        if kind == 0:
            src, dst = u_ref.at[to_core, :, part(to_q, cw)], ubuf.at[1 + t]
        elif kind == 1:
            src, dst = med_ref.at[:, part(to_q, ci)], mbuf.at[t]
        else:
            src, dst = b_ref.at[to_core, :, part(to_q, ci)], bbuf.at[t]
        return pltpu.make_async_remote_copy(
            src_ref=src, dst_ref=dst, send_sem=in_send.at[kind, there], recv_sem=in_recv.at[kind, t],
            device_id=(base + there,), device_id_type=MESH,
        )

    def in_wait(kind, there):
        dst = (ubuf.at[1 + there], mbuf.at[there], bbuf.at[there])[kind]
        pltpu.make_async_remote_copy(
            src_ref=dst, dst_ref=dst, send_sem=in_send.at[kind, there], recv_sem=in_recv.at[kind, there],
            device_id=(base + there,), device_id_type=MESH,
        ).wait_recv()

    others = [flip(t, d, bits) for d in range(planes - 1, 0, -1)]
    for kind in range(3):
        for there in others:
            in_copy(kind, there).start()
    ubuf[1 + t, :, :] = u_ref[core, :, part(q, cw)]
    mbuf[t, :, :] = med_ref[:, part(q, ci)]
    bbuf[t, :, :] = b_ref[core, :, part(q, ci)]

    shift = jnp.float32(0.0)
    for s in range(table_ref.shape[0]):
        shift = shift + jnp.where(index_ref[core] == s, table_ref[s], 0.0)
    shift = 6.0 + shift

    inner = pl.ds(LANES, ci)
    zero_plane = (0, planes + 1)
    for side in range(2):
        @pl.when(jnp.logical_not(has_z[side]))
        def _():
            ubuf[zero_plane[side]] = jnp.zeros(ubuf.shape[1:], jnp.float32)
            for j in range(STEPS):
                vbuf[j, zero_plane[side]] = jnp.zeros(vbuf.shape[2:], jnp.float32)

        @pl.when(jnp.logical_not(has_x[side]))
        def _():
            lanes = pl.ds((0, cw - LANES)[side], LANES)
            for j in range(STEPS):
                vbuf[j, :, :, lanes] = jnp.zeros((planes + 2, block, LANES), jnp.float32)

    def z_copy(stage, side):
        buf = ubuf if stage == 0 else vbuf.at[stage - 1]
        return pltpu.make_async_remote_copy(
            src_ref=buf.at[(1, planes)[side], :, inner], dst_ref=buf.at[(planes + 1, 0)[side], :, inner],
            send_sem=z_send.at[stage, side], recv_sem=z_recv.at[stage, side],
            device_id=(z_to[side],), device_id_type=MESH,
        )

    def x_copy(stage, side):
        buf = vbuf.at[stage - 1]
        mid = pl.ds(1, planes)
        return pltpu.make_async_remote_copy(
            src_ref=buf.at[mid, :, pl.ds((LANES, ci)[side], LANES)],
            dst_ref=buf.at[mid, :, pl.ds((cw - LANES, 0)[side], LANES)],
            send_sem=x_send.at[stage - 1, side], recv_sem=x_recv.at[stage - 1, side],
            device_id=(x_to[side],), device_id_type=MESH,
        )

    def both_sides(has, make, act):
        for side in range(2):
            @pl.when(has[side])
            def _():
                getattr(make(side), act)()

    def halo_start(has, make):
        both_sides(has, make, "start")

    def halo_wait(has, make):
        both_sides(has[::-1], make, "wait_recv")

    def reduce_sum(buffer, number, value):
        sem = number if buffer is gram0 else number + 1
        offset = 0
        for f, stride, mine, first in peers:
            own = offset + mine
            buffer[number, own, :, :] = value
            for d in range(1, f):
                to = lax.rem(mine + d, f)
                pltpu.make_async_remote_copy(
                    src_ref=buffer.at[number, own], dst_ref=buffer.at[number, own],
                    send_sem=red_send.at[sem, offset + d], recv_sem=red_recv.at[sem, own],
                    device_id=(first + to * stride,), device_id_type=MESH,
                ).start()
            for d in range(1, f):
                there = lax.rem(mine + d, f)
                origin = offset + there
                pltpu.make_async_remote_copy(
                    src_ref=buffer.at[number, origin], dst_ref=buffer.at[number, origin],
                    send_sem=red_send.at[sem, offset + d], recv_sem=red_recv.at[sem, origin],
                    device_id=(first + there * stride,), device_id_type=MESH,
                ).wait_recv()
            value = buffer[number, offset, :, :]
            for s in range(1, f):
                value = value + buffer[number, offset + s, :, :]
            offset += f
        return value

    def reduce_drain(buffer, number):
        sem = number if buffer is gram0 else number + 1
        offset = 0
        for f, stride, mine, first in peers:
            for d in range(1, f):
                pltpu.make_async_remote_copy(
                    src_ref=buffer.at[number, offset + mine], dst_ref=buffer.at[number, offset + mine],
                    send_sem=red_send.at[sem, offset + d], recv_sem=red_recv.at[sem, offset + mine],
                    device_id=(first + lax.rem(mine + d, f) * stride,), device_id_type=MESH,
                ).wait_send()
            offset += f

    lane = iota2((1, LANES), 1)

    def stencil(buf, p, tile):
        load = lambda z, s: buf[z, :, s * LANES : (s + 1) * LANES]
        c = load(p + 1, tile + 1)
        near = load(p + 1, tile) + load(p + 1, tile + 2)
        near = near + load(p, tile + 1) + load(p + 2, tile + 1)
        near = near + jnp.where(lane == 0, 0.0, pltpu.roll(c, 1, 1))
        near = near + jnp.where(lane == LANES - 1, 0.0, pltpu.roll(c, LANES - 1, 1))
        diag = mbuf[p, :, tile * LANES : (tile + 1) * LANES] + shift
        return diag * c - near, c

    def put(high, low, p, row, tile, value):
        at = slice(tile * LANES, (tile + 1) * LANES)
        h, l = halves(value)
        high[p, row : row + value.shape[0], at] = h
        low[p, row : row + value.shape[0], at] = l

    for kind in range(2):
        for there in others:
            in_wait(kind, there)
    halo_start(has_z, lambda side: z_copy(0, side))

    fill = jnp.zeros((pad - k_rows, LANES), jnp.float32)

    def widen(x):
        return jnp.concatenate([x, fill], axis=0) if pad > k_rows else x

    def image_plane(p, carry):
        for tile in range(tiles):
            applied, c = stencil(ubuf, p, tile)
            put(sh, sl, p, 0, tile, widen(applied))
            put(uh, ul, p, 0, tile, widen(c))
        return carry

    if planes > 2:
        lax.fori_loop(1, planes - 1, image_plane, 0)
    halo_wait(has_z, lambda side: z_copy(0, side))
    image_plane(0, 0)
    image_plane(planes - 1, 0)

    for there in others:
        in_wait(2, there)
    size = pad + block

    def first_gram(p, acc):
        for tile in range(tiles):
            put(sh, sl, p, pad, tile, bbuf[p, :, tile * LANES : (tile + 1) * LANES])
        rows = sh[p, 0:size, :]
        return acc + one_t(jnp.concatenate([rows, sl[p, 0:size, :]], axis=0), rows)

    acc = lax.fori_loop(0, planes, first_gram, jnp.zeros((2 * size, size), jnp.float32))
    cross = acc[size:, :]
    whole = acc[:size, :] + cross + dot_t(eye(size), cross)
    fin[0:k_rows, 0:size] = whole[0:k_rows, :]
    fin[0:k_rows, size:] = jnp.zeros((k_rows, LANES - size), jnp.float32)
    half = LANES // 2
    fin[0:block, half : half + block] = whole[pad:, pad:]
    fin[0:k_rows, :] = reduce_sum(gram0, 0, fin[0:k_rows, :])
    if pad > k_rows:
        fin[k_rows:pad, :] = jnp.zeros((pad - k_rows, LANES), jnp.float32)
    linv = factor(fin[0:pad, 0:pad], k_rows)[1]
    proj_t = dot_t(dot_t(eye(block), fin[0:pad, pad:size]), linv)
    remaining = fin[0:block, half : half + block] - dot_t(proj_t, proj_t)
    top_factor, inv = factor(remaining, block)
    coef[:, 0:pad] = -dot(inv, dot(proj_t, linv))
    coef[:, pad:size] = inv
    hbt[...] = jnp.zeros(hbt.shape, jnp.float32)

    unit = eye(block)
    for j in range(1, STEPS + 1):
        known = pad + block * j
        stacked = jnp.concatenate(thirds(coef[:, 0:known]), axis=0)

        def combine_plane(p, carry):
            first = one(stacked, sh[p, 0:known, :])
            second = one(stacked[0 : 2 * block], sl[p, 0:known, :])
            value = first[0:block] + (first[block : 2 * block] + second[0:block])
            value = value + (first[2 * block :] + second[block:])
            vbuf[j - 1, p + 1, :, inner] = value
            for tile in range(tiles):
                put(sh, sl, p, known - block, tile, value[:, tile * LANES : (tile + 1) * LANES])
            return carry

        combine_plane(0, 0)
        combine_plane(planes - 1, 0)
        halo_start(has_z, lambda side: z_copy(j, side))
        if planes > 2:
            lax.fori_loop(1, planes - 1, combine_plane, 0)
        halo_start(has_x, lambda side: x_copy(j, side))
        halo_wait(has_z, lambda side: z_copy(j, side))
        halo_wait(has_x, lambda side: x_copy(j, side))
        wide = known + block

        def gram_plane(p, acc):
            for tile in range(tiles):
                put(sh, sl, p, known, tile, stencil(vbuf.at[j - 1], p, tile)[0])
            rows, rest = sh[p, 0:wide, :], sl[p, 0:wide, :]
            new = jnp.concatenate([rows[known:], rest[known:]], axis=0)
            return acc + one_t(jnp.concatenate([rows, rest], axis=0), new)

        acc = lax.fori_loop(0, planes, gram_plane, jnp.zeros((2 * wide, 2 * block), jnp.float32))
        tall = acc[0:wide, 0:block] + (acc[wide:, 0:block] + acc[0:wide, block:] + acc[wide:, block:])
        fin[0:block, 0:wide] = dot_t(unit, tall)
        fin[0:block, :] = reduce_sum(gram, j - 1, fin[0:block, :])
        et = dot_t(fin[0:block, 0:pad], linv)
        ht = fin[0:block, pad:known]
        fresh = fin[0:block, known:wide] - dot_t(et, et) - dot_t(ht, ht)
        lt, inv = factor(fresh, block)
        coef[:, 0:pad] = -dot(inv, dot(et, linv))
        coef[:, pad:known] = -dot(inv, ht)
        coef[:, known:wide] = inv
        at = block * (j - 1)
        hbt[at : at + block, 0 : known - pad] = ht
        hbt[at : at + block, known - pad : known - pad + block] = dot_t(unit, lt)
        ebt[at : at + block, :] = et

    width = pad + block * (STEPS + 1)
    kry = block * STEPS
    h = hbt[:, 0 : kry + block]
    ys = solve(dot_t(h, h), dot(hbt[:, 0:block], top_factor))
    yt = dot_t(unit, ys)
    back[...] = dot(proj_t - dot(yt, ebt[...]), linv)
    fin[0:block, :] = -dot(yt, hbt[...])
    fin[0:block, 0:block] = fin[0:block, 0:block] + dot_t(unit, top_factor)
    top = fin[0:block, 0:kry]
    last = dot(fin[0:block, kry : kry + block], coef[:, 0:width])
    fin[...] = jnp.zeros(fin.shape, jnp.float32)
    fin[0:block, pad : pad + kry] = yt
    fin[block : 2 * block, 0:width] = last
    fin[block : 2 * block, pad : pad + kry] = fin[block : 2 * block, pad : pad + kry] + top
    high, low = halves(fin[0 : 2 * block, 0:width])
    stacked = jnp.concatenate([high, low], axis=0)
    bh, bl = halves(back[...])
    bstack = jnp.concatenate([bh, bl], axis=0)

    def out_copy(kind, there):
        dst = (sol_ref, res_ref)[kind]
        return pltpu.make_async_remote_copy(
            src_ref=obuf.at[there, pl.ds(kind * block, block)], dst_ref=dst.at[core, :, part(q, ci)],
            send_sem=out_send.at[kind, there], recv_sem=out_recv.at[kind, t],
            device_id=(base + there,), device_id_type=MESH,
        )

    def out_wait(kind, there):
        dst = (sol_ref, res_ref)[kind].at[lax.rem(there, 2), :, part(gray(there // 2), ci)]
        pltpu.make_async_remote_copy(
            src_ref=dst, dst_ref=dst, send_sem=out_send.at[kind, there], recv_sem=out_recv.at[kind, there],
            device_id=(base + there,), device_id_type=MESH,
        ).wait_recv()

    def final_plane(p):
        first = one(stacked, sh[p, 0:width, :])
        both = first[0 : 2 * block] + (first[2 * block :] + one(high, sl[p, 0:width, :]))
        first = one(bstack, uh[p])
        return both[0:block] + (first[0:block] + (first[block:] + one(bh, ul[p]))), both[block:]

    def final_send(i, carry):
        there = flip(t, planes - 1 - i, bits)
        sol, res = final_plane(there)
        obuf[there, 0:block, :] = sol
        obuf[there, block:, :] = res
        for kind in range(2):
            out_copy(kind, there).start()
        return carry

    lax.fori_loop(0, planes - 1, final_send, 0)
    sol, res = final_plane(t)
    sol_ref[core, :, part(q, ci)] = sol
    res_ref[core, :, part(q, ci)] = res

    for kind in range(3):
        for there in others:
            in_copy(kind, there).wait_send()
    for stage in range(STEPS + 1):
        both_sides(has_z, lambda side: z_copy(stage, side), "wait_send")
        if stage:
            both_sides(has_x, lambda side: x_copy(stage, side), "wait_send")
    reduce_drain(gram0, 0)
    for j in range(STEPS):
        reduce_drain(gram, j)
    for there in others:
        for kind in range(2):
            out_wait(kind, there)
            out_copy(kind, there).wait_send()


def split_count(n):
    out = []
    while n > 1:
        f = next(f for f in (4, 2, 8, n) if n % f == 0)
        out.append(f)
        n //= f
    return out


def solution(mesh):
    n = mesh.shape["grid"]

    def on_device(right_sides, recycle, medium, shift_table, shift_index):
        block = right_sides.shape[0] // 2
        k_rows = recycle.shape[1]
        lines = right_sides.shape[2]
        cells = lines * right_sides.shape[3]
        quarters = next(q for q in (4, 2, 1) if n % (2 * q) == 0 and lines % q == 0)
        planes = 2 * quarters
        stages, stride = [], 2
        for count in (quarters, n // planes):
            for f in split_count(count):
                stages.append((f, stride))
                stride *= f
        pad = -(-k_rows // block) * block
        ci = cells // quarters
        cw = ci + 2 * LANES
        width = pad + block * (STEPS + 1)
        b = right_sides.reshape(2, block, cells)
        u = jnp.pad(recycle.reshape(2, k_rows, cells), ((0, 0), (0, 0), (LANES, LANES)))
        slots = sum(f for f, _ in stages)
        vmem = pl.BlockSpec(memory_space=pltpu.VMEM)
        smem = pl.BlockSpec(memory_space=pltpu.SMEM)
        shape = jax.ShapeDtypeStruct((2, block, cells), jnp.float32)
        f32, half = jnp.float32, jnp.bfloat16
        sems = lambda *s: pltpu.SemaphoreType.DMA(s)
        sol, res = pl.pallas_call(
            functools.partial(kernel, n, quarters, tuple(stages)),
            out_shape=(shape, shape),
            in_specs=[vmem, vmem, vmem, smem, smem],
            out_specs=(vmem, vmem),
            scratch_shapes=[
                pltpu.VMEM((planes + 2, k_rows, cw), f32),
                pltpu.VMEM((STEPS, planes + 2, block, cw), f32),
                pltpu.VMEM((planes, block, ci), f32),
                pltpu.VMEM((planes, 1, ci), f32),
                pltpu.VMEM((planes, width, ci), half),
                pltpu.VMEM((planes, width, ci), half),
                pltpu.VMEM((planes, pad, ci), half),
                pltpu.VMEM((planes, pad, ci), half),
                pltpu.VMEM((planes, 2 * block, ci), f32),
                pltpu.VMEM((1, slots, k_rows, LANES), f32),
                pltpu.VMEM((STEPS, slots, block, LANES), f32),
                pltpu.VMEM((block, LANES), f32),
                pltpu.VMEM((block * STEPS, LANES), f32),
                pltpu.VMEM((block * STEPS, pad), f32),
                pltpu.VMEM((pad, LANES), f32),
                pltpu.VMEM((block, pad), f32),
                sems(3, planes), sems(3, planes),
                sems(STEPS + 1, 2), sems(STEPS + 1, 2),
                sems(STEPS, 2), sems(STEPS, 2),
                sems(STEPS + 1, slots), sems(STEPS + 1, slots),
                sems(2, planes), sems(2, planes),
            ],
            compiler_params=pltpu.CompilerParams(
                collective_id=0, has_side_effects=True, vmem_limit_bytes=48 * 1024 * 1024
            ),
        )(u, b, medium.reshape(1, cells), shift_table, shift_index)
        return sol.reshape(right_sides.shape), res.reshape(right_sides.shape)

    rows = P(None, "grid", None, None)
    return jax.shard_map(
        on_device,
        mesh=mesh,
        in_specs=(rows, P(None, None, "grid", None, None), P("grid", None, None), P(), P()),
        out_specs=(rows, rows),
        check_vma=False,
    )
```

time: 155 us -> 123 us (0.79)
  Pallas kernels: 149 us -> 118 us
    pallas_call x1, Pallas kernels: 149 us -> 118 us  [on_device(): pl.pallas_call(functools.partial(kernel, n, quarters, tuple(stages)), out...]
where the time goes in v1:
time: 123 us
  Pallas kernels  118 us (96%)
  local copies, waits for them, and re-layouts  4.43 us (4%)
    pallas_call x1, Pallas kernels, on_device(): pl.pallas_call(functools.partial(kernel, n, quarters, tuple(stages)), out...  118 us
    unnamed x10, local copies, waits for them, and re-layouts  2.82 us

profile of v1, /device:TPU:0, one launch (start us, length us, event | category | flops | bytes accessed | tf_op | source)
XLA Modules:
  0.0 122.8 jit_solution(10400032606944540652)
XLA Ops:
  0.6 0.0 copy-start.3
  0.6 1.4 %reshape.20.b_ref = f32[2,16,6144]{2,1,0:T(8,128)S(1)} reshape(f32[32,1,48,128]{3,2,1,0:T(8,128)} %param.5) | data formatting | bytes 1572864 | tf_op jit(solution)/shard_map/reshape | solution.py:478
  2.0 0.1 copy-done.3
  2.1 0.2 reshape.19
  2.3 0.0 copy-start
  2.3 0.0 copy-start.1
  2.3 0.0 copy-start.2
  2.4 0.1 pad.4.u_ref
  2.4 0.6 copy-done
  3.1 0.0 copy-done.1
  3.1 0.0 copy-done.2
  3.1 117.7 %shard_map.68 = (f32[2,16,6144]{2,1,0:T(8,128)S(1)}, f32[2,16,6144]{2,1,0:T(8,128)S(1)}) custom-call(f32[2,24,6400]{2,1,0:T(8,128)S(1)} %pad.4.u_ref, f32[2,16,6144]{2,1,0:T(8,128)S(1)} %reshape.20.b_ref, f32[1,6144]{1,0:T(1,128)S(1)} %bitcast.21, f32[8]{0:T(128)S(1)} %copy-done.1, s32[2]{0:T(128)S(1)} %copy-done.2), custom_call_target="tpu_custom_call" | custom-call | tf_op jit(solution)/shard_map/pallas_call | solution.py:486
  120.8 1.0 copy.9
  121.8 1.0 copy.10
Async XLA Ops:
  0.6 1.5 %copy-start.3 = (f32[2,24,1,48,128]{4,3,2,1,0:T(8,128)S(1)}, f32[2,24,1,48,128]{4,3,2,1,0:T(8,128)}, u32[]{:S(2)}) copy-start(f32[2,24,1,48,128]{4,3,2,1,0:T(8,128)} %param.6) | copy-start | bytes 3538948
  2.3 0.7 copy-start
  2.3 0.7 copy-start.1
  2.3 0.7 copy-start.2

commit v2 on v1

--- a/solution.py
+++ b/solution.py
@@ -51,42 +51,44 @@
     return jnp.where(iota2((size, size), 0) == iota2((size, size), 1), 1.0, 0.0)
 
 
-def pair_step(arrays, k, first, second):
-    c1, c2 = arrays[0][:, k : k + 1], arrays[0][:, k + 1 : k + 2]
-    f1 = jnp.where(first, c1 * (1.0 / c1[k : k + 1]), 0.0)
-    c2 = c2 - f1 * c2[k : k + 1]
-    f2 = jnp.where(second, c2 * (1.0 / c2[k + 1 : k + 2]), 0.0)
-    link = f1[k + 1 : k + 2]
-    out = []
-    for x in arrays:
-        r1 = x[k : k + 1, :]
-        r2 = x[k + 1 : k + 2, :] - link * r1
-        out.append(x - f1 * r1 - f2 * r2)
-    return tuple(out)
-
-
-def factor(matrix, count):
+def pair_step(x, k, first, second):
+    b1 = jnp.broadcast_to(x[:, k : k + 1], x.shape)
+    b2 = jnp.broadcast_to(x[:, k + 1 : k + 2], x.shape)
+    p12 = b2[k : k + 1]
+    i1 = 1.0 / b1[k : k + 1]
+    link = b1[k + 1 : k + 2] * i1
+    i2 = 1.0 / (b2[k + 1 : k + 2] - link * p12)
+    f1 = jnp.where(first, b1 * i1, 0.0)
+    f2 = jnp.where(second, (b2 - f1 * p12) * i2, 0.0)
+    r1 = x[k : k + 1, :]
+    r2 = x[k + 1 : k + 2, :] - link * r1
+    return x - f1 * r1 - f2 * r2
+
+
+def beside(matrix, offset):
     size = matrix.shape[0]
+    shape = (size, LANES)
+    return jnp.where(iota2(shape, 1) == iota2(shape, 0) + offset, 1.0, matrix)
+
+
+def factor(x, size, count):
     rows = iota2((size, 1), 0)
-    unit = jnp.where(rows < count, eye(size), 0.0)
-    parts = (matrix, unit)
+    diagonal = iota2((size, LANES), 1) == rows
     for k in range(0, count, 2):
-        parts = pair_step(parts, k, rows > k, rows > k + 1)
-    a, z = parts
+        x = pair_step(x, k, rows > k, rows > k + 1)
+    pivots = jnp.sum(jnp.where(diagonal, x, 0.0), axis=1, keepdims=True)
+    root = jnp.where(rows < count, lax.rsqrt(jnp.where(rows < count, pivots, 1.0)), 0.0)
+    x = x * root
     upper = iota2((size, size), 1) >= iota2((size, size), 0)
-    pivots = jnp.sum(a * unit, axis=1, keepdims=True)
-    root = jnp.where(rows < count, lax.rsqrt(jnp.where(rows < count, pivots, 1.0)), 0.0)
-    return jnp.where(upper, a * root, 0.0), z * root
-
-
-def solve(matrix, right):
-    size = matrix.shape[0]
+    return jnp.where(upper, x[:, 0:size], 0.0), x[:, size : 2 * size]
+
+
+def eliminate(x, size):
     rows = iota2((size, 1), 0)
-    parts = (matrix, right)
     for k in range(0, size, 2):
-        parts = pair_step(parts, k, rows != k, rows != k + 1)
-    a, r = parts
-    return r / jnp.sum(a * eye(size), axis=1, keepdims=True)
+        x = pair_step(x, k, rows != k, rows != k + 1)
+    diagonal = iota2((size, LANES), 1) == rows
+    return x / jnp.sum(jnp.where(diagonal, x, 0.0), axis=1, keepdims=True)
 
 
 def gray(j):
@@ -102,13 +104,22 @@
 
 def kernel(
     n, quarters, stages,
-    u_ref, b_ref, med_ref, table_ref, index_ref, sol_ref, res_ref,
-    ubuf, vbuf, bbuf, mbuf, sh, sl, uh, ul, obuf, gram0, gram, coef, hbt, ebt, fin, back,
-    in_send, in_recv, z_send, z_recv, x_send, x_recv, red_send, red_recv, out_send, out_recv,
+    u_hbm, b_hbm, med_hbm, table_hbm, index_hbm, sol_lines, res_lines,
+    u_lines, b_lines, med_ref, table_ref, index_ref,
+    u_ref, b_ref, sol_ref, res_ref, ubuf, vbuf, bbuf, mbuf, sh, sl, uh, ul, obuf, gram0, gram, coef, hbt, ebt, lsq, fin, back,
+    in_sem, in_send, in_recv, z_send, z_recv, x_send, x_recv, red_send, red_recv, out_send, out_recv,
 ):
     me = lax.axis_index("grid")
     planes = 2 * quarters
     bits = planes.bit_length() - 1
+    takes = [
+        pltpu.make_async_copy(src, dst, in_sem.at[i])
+        for i, (src, dst) in enumerate((
+            (u_hbm, u_lines), (b_hbm, b_lines), (med_hbm, med_ref), (table_hbm, table_ref), (index_hbm, index_ref)
+        ))
+    ]
+    for take in takes:
+        take.start()
     k_rows = u_ref.shape[1]
     block = b_ref.shape[1]
     cells = b_ref.shape[2]
@@ -132,12 +143,33 @@
         peers.append((f, stride, mine, me - mine * stride))
     greet = [base + flip(t, d, bits) for d in range(1, planes)]
     for f, stride, mine, first in peers:
-        if stride >= planes:
-            greet += [first + lax.rem(mine + d, f) * stride for d in range(1, f)]
+        greet += [first + lax.rem(mine + d, f) * stride for d in range(1, f)]
     if layers > 1:
         greet += [lax.rem(me + planes, n), lax.rem(me + n - planes, n)]
     for to in greet:
         pl.semaphore_signal(barrier, inc=1, device_id=(to,), device_id_type=MESH)
+
+    lines = cells // LANES
+    for g in range(2):
+        u_ref[g, :, 0:LANES] = jnp.zeros((k_rows, LANES), jnp.float32)
+        u_ref[g, :, cells + LANES :] = jnp.zeros((k_rows, LANES), jnp.float32)
+
+    def take_u(x, carry):
+        after = pl.ds(pl.multiple_of(x * LANES + LANES, LANES), LANES)
+        for g in range(2):
+            u_ref[g, :, after] = u_lines[g, :, x, :]
+        return carry
+
+    def take_b(x, carry):
+        at = pl.ds(pl.multiple_of(x * LANES, LANES), LANES)
+        for g in range(2):
+            b_ref[g, :, at] = b_lines[g, :, x, :]
+        return carry
+
+    takes[0].wait()
+    lax.fori_loop(0, lines, take_u, 0, unroll=4)
+    for take in takes[1:]:
+        take.wait()
     pl.semaphore_wait(barrier, len(greet))
 
     def part(qq, width):
@@ -164,9 +196,13 @@
         ).wait_recv()
 
     others = [flip(t, d, bits) for d in range(planes - 1, 0, -1)]
-    for kind in range(3):
+    for kind in range(2):
         for there in others:
             in_copy(kind, there).start()
+
+    lax.fori_loop(0, lines, take_b, 0, unroll=4)
+    for there in others:
+        in_copy(2, there).start()
     ubuf[1 + t, :, :] = u_ref[core, :, part(q, cw)]
     mbuf[t, :, :] = med_ref[:, part(q, ci)]
     bbuf[t, :, :] = b_ref[core, :, part(q, ci)]
@@ -221,7 +257,7 @@
     def halo_wait(has, make):
         both_sides(has[::-1], make, "wait_recv")
 
-    def reduce_sum(buffer, number, value):
+    def reduce_sum(buffer, number, value, meanwhile=None):
         sem = number if buffer is gram0 else number + 1
         offset = 0
         for f, stride, mine, first in peers:
@@ -234,6 +270,9 @@
                     send_sem=red_send.at[sem, offset + d], recv_sem=red_recv.at[sem, own],
                     device_id=(first + to * stride,), device_id_type=MESH,
                 ).start()
+            if meanwhile is not None:
+                meanwhile()
+                meanwhile = None
             for d in range(1, f):
                 there = lax.rem(mine + d, f)
                 origin = offset + there
@@ -311,80 +350,154 @@
         rows = sh[p, 0:size, :]
         return acc + one_t(jnp.concatenate([rows, sl[p, 0:size, :]], axis=0), rows)
 
-    acc = lax.fori_loop(0, planes, first_gram, jnp.zeros((2 * size, size), jnp.float32))
+    acc = lax.fori_loop(0, planes, first_gram, jnp.zeros((2 * size, size), jnp.float32), unroll=min(4, planes))
     cross = acc[size:, :]
     whole = acc[:size, :] + cross + dot_t(eye(size), cross)
     fin[0:k_rows, 0:size] = whole[0:k_rows, :]
     fin[0:k_rows, size:] = jnp.zeros((k_rows, LANES - size), jnp.float32)
     half = LANES // 2
     fin[0:block, half : half + block] = whole[pad:, pad:]
-    fin[0:k_rows, :] = reduce_sum(gram0, 0, fin[0:k_rows, :])
+
+    def clear():
+        hbt[...] = jnp.zeros(hbt.shape, jnp.float32)
+        lsq[...] = jnp.zeros(lsq.shape, jnp.float32)
+
+    fin[0:k_rows, :] = reduce_sum(gram0, 0, fin[0:k_rows, :], clear)
     if pad > k_rows:
         fin[k_rows:pad, :] = jnp.zeros((pad - k_rows, LANES), jnp.float32)
-    linv = factor(fin[0:pad, 0:pad], k_rows)[1]
-    proj_t = dot_t(dot_t(eye(block), fin[0:pad, pad:size]), linv)
-    remaining = fin[0:block, half : half + block] - dot_t(proj_t, proj_t)
-    top_factor, inv = factor(remaining, block)
-    coef[:, 0:pad] = -dot(inv, dot(proj_t, linv))
+    lanes = iota2((pad, LANES), 1)
+    mixed = fin[0:pad, 0:size]
+    linv = factor(beside(jnp.where(lanes < pad, fin[0:pad, :], 0.0), pad), pad, k_rows)[1]
+    whole_inv = lax.dot_general(
+        linv, linv, (((0,), (0,)), ((), ())), precision=highest, preferred_element_type=jnp.float32
+    )
+    ba = dot_t(eye(block), mixed[:, pad:size])
+    ba_inv = dot(ba, whole_inv)
+    remaining = fin[0:block, half : half + block] - dot_t(ba_inv, ba)
+    wide_zero = jnp.zeros((block, LANES - block), jnp.float32)
+    full = lambda m: jnp.concatenate([m, wide_zero], axis=1)
+    top_factor, inv = factor(beside(full(remaining), block), block, block)
+    coef[:, 0:pad] = -dot(inv, ba_inv)
     coef[:, pad:size] = inv
-    hbt[...] = jnp.zeros(hbt.shape, jnp.float32)
 
     unit = eye(block)
+    lower = dot_t(unit, top_factor)
     for j in range(1, STEPS + 1):
         known = pad + block * j
         stacked = jnp.concatenate(thirds(coef[:, 0:known]), axis=0)
 
-        def combine_plane(p, carry):
-            first = one(stacked, sh[p, 0:known, :])
-            second = one(stacked[0 : 2 * block], sl[p, 0:known, :])
+        def combine(p, first_tile, last_tile):
+            at = slice(first_tile * LANES, last_tile * LANES)
+            first = one(stacked, sh[p, 0:known, at])
+            second = one(stacked[0 : 2 * block], sl[p, 0:known, at])
             value = first[0:block] + (first[block : 2 * block] + second[0:block])
             value = value + (first[2 * block :] + second[block:])
-            vbuf[j - 1, p + 1, :, inner] = value
+            vbuf[j - 1, p + 1, :, LANES + first_tile * LANES : LANES + last_tile * LANES] = value
+            for tile in range(first_tile, last_tile):
+                here = slice((tile - first_tile) * LANES, (tile - first_tile + 1) * LANES)
+                put(sh, sl, p, known - block, tile, value[:, here])
+
+        def combine_edges(p, carry):
+            combine(p, 0, 1)
+            combine(p, tiles - 1, tiles)
+            return carry
+
+        def combine_inner(p, carry):
+            combine(p, 1, tiles - 1)
+            return carry
+
+        def image_inner(p, carry):
+            for tile in range(1, tiles - 1):
+                put(sh, sl, p, known, tile, stencil(vbuf.at[j - 1], p, tile)[0])
+            return carry
+
+        wide = known + block
+        ends = (0, planes - 1)
+        acc = jnp.zeros((2 * wide, 2 * block), jnp.float32)
+
+        def gram_of(rows, rest):
+            new = jnp.concatenate([rows[known:], rest[known:]], axis=0)
+            return one_t(jnp.concatenate([rows, rest], axis=0), new)
+
+        def image(p, tile):
+            put(sh, sl, p, known, tile, stencil(vbuf.at[j - 1], p, tile)[0])
+
+        def inner_gram(p, acc):
+            for tile in range(1, tiles - 1):
+                image(p, tile)
+            at = slice(LANES, (tiles - 1) * LANES)
+            return acc + gram_of(sh[p, 0:wide, at], sl[p, 0:wide, at])
+
+        for p in ends:
+            combine(p, 0, tiles)
+        halo_start(has_z, lambda side: z_copy(j, side))
+        for p in range(1, planes - 1):
+            combine(p, 0, 1)
+            combine(p, tiles - 1, tiles)
+        halo_start(has_x, lambda side: x_copy(j, side))
+        for p in range(1, planes - 1):
+            combine(p, 1, tiles - 1)
+        if planes > 2:
+            acc = lax.fori_loop(1, planes - 1, inner_gram, acc, unroll=(planes - 2) // 2)
+        halo_wait(has_x, lambda side: x_copy(j, side))
+        lanes_of = lambda ref, p, tile: ref[p, 0:wide, tile * LANES : (tile + 1) * LANES]
+        sides = [(p, tile) for p in range(1, planes - 1) for tile in (0, tiles - 1)]
+        for p, tile in sides:
+            image(p, tile)
+        if sides:
+            acc = acc + gram_of(*(
+                jnp.concatenate([lanes_of(ref, p, tile) for p, tile in sides], axis=1) for ref in (sh, sl)
+            ))
+        halo_wait(has_z, lambda side: z_copy(j, side))
+        for p in ends:
             for tile in range(tiles):
-                put(sh, sl, p, known - block, tile, value[:, tile * LANES : (tile + 1) * LANES])
-            return carry
-
-        combine_plane(0, 0)
-        combine_plane(planes - 1, 0)
-        halo_start(has_z, lambda side: z_copy(j, side))
-        if planes > 2:
-            lax.fori_loop(1, planes - 1, combine_plane, 0)
-        halo_start(has_x, lambda side: x_copy(j, side))
-        halo_wait(has_z, lambda side: z_copy(j, side))
-        halo_wait(has_x, lambda side: x_copy(j, side))
-        wide = known + block
-
-        def gram_plane(p, acc):
-            for tile in range(tiles):
-                put(sh, sl, p, known, tile, stencil(vbuf.at[j - 1], p, tile)[0])
-            rows, rest = sh[p, 0:wide, :], sl[p, 0:wide, :]
-            new = jnp.concatenate([rows[known:], rest[known:]], axis=0)
-            return acc + one_t(jnp.concatenate([rows, rest], axis=0), new)
-
-        acc = lax.fori_loop(0, planes, gram_plane, jnp.zeros((2 * wide, 2 * block), jnp.float32))
+                image(p, tile)
+            acc = acc + gram_of(sh[p, 0:wide, :], sl[p, 0:wide, :])
         tall = acc[0:wide, 0:block] + (acc[wide:, 0:block] + acc[0:wide, block:] + acc[wide:, block:])
         fin[0:block, 0:wide] = dot_t(unit, tall)
-        fin[0:block, :] = reduce_sum(gram, j - 1, fin[0:block, :])
-        et = dot_t(fin[0:block, 0:pad], linv)
+        early = block * (STEPS - 1)
+
+        if j == STEPS:
+            pads = jnp.zeros((early, LANES - early), jnp.float32)
+
+            def invert_early():
+                he = hbt[0:early, :]
+                normal = jnp.concatenate([dot_t(he, he), pads], axis=1)
+                lsq[...] = eliminate(beside(normal, early), early)
+
+            fin[0:block, :] = reduce_sum(gram, j - 1, fin[0:block, :], invert_early)
+        else:
+            fin[0:block, :] = reduce_sum(gram, j - 1, fin[0:block, :])
+        wa = fin[0:block, 0:pad]
+        wa_inv = dot(wa, whole_inv)
         ht = fin[0:block, pad:known]
-        fresh = fin[0:block, known:wide] - dot_t(et, et) - dot_t(ht, ht)
-        lt, inv = factor(fresh, block)
-        coef[:, 0:pad] = -dot(inv, dot(et, linv))
+        fresh = fin[0:block, known:wide] - dot_t(ht, ht) - dot_t(wa_inv, wa)
+        lt, inv = factor(beside(full(fresh), block), block, block)
+        coef[:, 0:pad] = -dot(inv, wa_inv)
         coef[:, pad:known] = -dot(inv, ht)
         coef[:, known:wide] = inv
         at = block * (j - 1)
         hbt[at : at + block, 0 : known - pad] = ht
         hbt[at : at + block, known - pad : known - pad + block] = dot_t(unit, lt)
-        ebt[at : at + block, :] = et
+        ebt[at : at + block, :] = wa_inv
 
     width = pad + block * (STEPS + 1)
     kry = block * STEPS
-    h = hbt[:, 0 : kry + block]
-    ys = solve(dot_t(h, h), dot(hbt[:, 0:block], top_factor))
-    yt = dot_t(unit, ys)
-    back[...] = dot(proj_t - dot(yt, ebt[...]), linv)
+    he, hl = hbt[0:early, :], hbt[early:kry, :]
+    p = lsq[:, early : 2 * early]
+    rt_early = dot_t(lower, he[:, 0:block])
+    rt_late = dot_t(lower, hl[:, 0:block])
+    cross = dot_t(hl, he)
+    bent = dot(cross, p)
+    schur = dot_t(hl, hl) - dot_t(bent, cross)
+    yt0 = dot(rt_early, p)
+    late_right = rt_late - dot_t(yt0, cross)
+    both = jnp.concatenate([schur, dot_t(unit, late_right), wide_zero[:, block:]], axis=1)
+    y_late = dot_t(unit, eliminate(both, block)[:, block : 2 * block])
+    yt = jnp.concatenate([yt0 - dot(y_late, bent), y_late], axis=1)
+    back[...] = ba_inv - dot(yt, ebt[...])
     fin[0:block, :] = -dot(yt, hbt[...])
-    fin[0:block, 0:block] = fin[0:block, 0:block] + dot_t(unit, top_factor)
+    fin[0:block, 0:block] = fin[0:block, 0:block] + lower
     top = fin[0:block, 0:kry]
     last = dot(fin[0:block, kry : kry + block], coef[:, 0:width])
     fin[...] = jnp.zeros(fin.shape, jnp.float32)
@@ -428,9 +541,18 @@
 
     lax.fori_loop(0, planes - 1, final_send, 0)
     sol, res = final_plane(t)
-    sol_ref[core, :, part(q, ci)] = sol
-    res_ref[core, :, part(q, ci)] = res
-
+    for x in range(tiles):
+        sol_lines[core, :, q * tiles + x, :] = sol[:, x * LANES : (x + 1) * LANES]
+        res_lines[core, :, q * tiles + x, :] = res[:, x * LANES : (x + 1) * LANES]
+
+    for there in others:
+        g, first_line = lax.rem(there, 2), gray(there // 2) * tiles
+        for kind in range(2):
+            out_wait(kind, there)
+            landed, lines_of = (sol_ref, sol_lines, res_ref, res_lines)[2 * kind : 2 * kind + 2]
+            for x in range(tiles):
+                at = pl.ds(pl.multiple_of((first_line + x) * LANES, LANES), LANES)
+                lines_of[g, :, first_line + x, :] = landed[g, :, at]
     for kind in range(3):
         for there in others:
             in_copy(kind, there).wait_send()
@@ -443,14 +565,13 @@
         reduce_drain(gram, j)
     for there in others:
         for kind in range(2):
-            out_wait(kind, there)
             out_copy(kind, there).wait_send()
 
 
 def split_count(n):
     out = []
     while n > 1:
-        f = next(f for f in (4, 2, 8, n) if n % f == 0)
+        f = next(f for f in (16, 8, 4, 2, n) if n % f == 0)
         out.append(f)
         n //= f
     return out
@@ -467,28 +588,36 @@
         quarters = next(q for q in (4, 2, 1) if n % (2 * q) == 0 and lines % q == 0)
         planes = 2 * quarters
         stages, stride = [], 2
-        for count in (quarters, n // planes):
-            for f in split_count(count):
-                stages.append((f, stride))
-                stride *= f
+        for f in split_count(n // 2):
+            stages.append((f, stride))
+            stride *= f
         pad = -(-k_rows // block) * block
         ci = cells // quarters
         cw = ci + 2 * LANES
         width = pad + block * (STEPS + 1)
-        b = right_sides.reshape(2, block, cells)
-        u = jnp.pad(recycle.reshape(2, k_rows, cells), ((0, 0), (0, 0), (LANES, LANES)))
+        b = right_sides.reshape(2, block, lines, right_sides.shape[3])
+        u = recycle.reshape(2, k_rows, lines, right_sides.shape[3])
         slots = sum(f for f, _ in stages)
         vmem = pl.BlockSpec(memory_space=pltpu.VMEM)
-        smem = pl.BlockSpec(memory_space=pltpu.SMEM)
-        shape = jax.ShapeDtypeStruct((2, block, cells), jnp.float32)
+        hbm = pl.BlockSpec(memory_space=pltpu.HBM)
+        shape = jax.ShapeDtypeStruct(b.shape, jnp.float32)
         f32, half = jnp.float32, jnp.bfloat16
         sems = lambda *s: pltpu.SemaphoreType.DMA(s)
         sol, res = pl.pallas_call(
             functools.partial(kernel, n, quarters, tuple(stages)),
             out_shape=(shape, shape),
-            in_specs=[vmem, vmem, vmem, smem, smem],
+            in_specs=[hbm] * 5,
             out_specs=(vmem, vmem),
             scratch_shapes=[
+                pltpu.VMEM(u.shape, f32),
+                pltpu.VMEM(b.shape, f32),
+                pltpu.VMEM((1, cells), f32),
+                pltpu.SMEM(shift_table.shape, f32),
+                pltpu.SMEM(shift_index.shape, jnp.int32),
+                pltpu.VMEM((2, k_rows, cells + 2 * LANES), f32),
+                pltpu.VMEM((2, block, cells), f32),
+                pltpu.VMEM((2, block, cells), f32),
+                pltpu.VMEM((2, block, cells), f32),
                 pltpu.VMEM((planes + 2, k_rows, cw), f32),
                 pltpu.VMEM((STEPS, planes + 2, block, cw), f32),
                 pltpu.VMEM((planes, block, ci), f32),
@@ -503,8 +632,10 @@
                 pltpu.VMEM((block, LANES), f32),
                 pltpu.VMEM((block * STEPS, LANES), f32),
                 pltpu.VMEM((block * STEPS, pad), f32),
+                pltpu.VMEM((block * (STEPS - 1), LANES), f32),
                 pltpu.VMEM((pad, LANES), f32),
                 pltpu.VMEM((block, pad), f32),
+                sems(5),
                 sems(3, planes), sems(3, planes),
                 sems(STEPS + 1, 2), sems(STEPS + 1, 2),
                 sems(STEPS, 2), sems(STEPS, 2),
@@ -512,7 +643,7 @@
                 sems(2, planes), sems(2, planes),
             ],
             compiler_params=pltpu.CompilerParams(
-                collective_id=0, has_side_effects=True, vmem_limit_bytes=48 * 1024 * 1024
+                collective_id=0, has_side_effects=True, vmem_limit_bytes=65000000
             ),
         )(u, b, medium.reshape(1, cells), shift_table, shift_index)
         return sol.reshape(right_sides.shape), res.reshape(right_sides.shape)

time: 123 us -> 103 us (0.84)
  Pallas kernels: 118 us -> 99.4 us
  local copies, waits for them, and re-layouts: 4.43 us -> 3.02 us
    pallas_call x1, Pallas kernels: 118 us -> 99.4 us  [on_device(): pl.pallas_call(functools.partial(kernel, n, quarters, tuple(stages)), out...]
    reshape x2 -> x0, local copies, waits for them, and re-layouts: 1.53 us -> none  [the longest x1 1.35 us: on_device(): b = right_sides.reshape(2, block, cells)]
    unnamed x10 -> x4, local copies, waits for them, and re-layouts: 2.82 us -> 3.02 us
where the time goes in v2:
time: 103 us
  Pallas kernels  99.4 us (97%)
  local copies, waits for them, and re-layouts  3.02 us (3%)
    pallas_call x1, Pallas kernels, on_device(): pl.pallas_call(functools.partial(kernel, n, quarters, tuple(stages)), out...  99.4 us
    unnamed x4, local copies, waits for them, and re-layouts  3.02 us

profile of v2, /device:TPU:0, one launch (start us, length us, event | category | flops | bytes accessed | tf_op | source)
XLA Modules:
  0.0 103.0 jit_solution(10436432984060095784)
XLA Ops:
  0.6 99.4 %shard_map.68 = (f32[2,16,48,128]{3,2,1,0:T(8,128)}, f32[2,16,48,128]{3,2,1,0:T(8,128)}) custom-call(f32[2,24,48,128]{3,2,1,0:T(8,128)} %bitcast.9, f32[2,16,48,128]{3,2,1,0:T(8,128)} %bitcast.10, f32[1,6144]{1,0:T(1,128)} %bitcast.13, f32[8]{0:T(128)} %table_hbm.1, s32[2]{0:T(128)} %index_hbm.1), custom_call_target="tpu_custom_call" | custom-call | tf_op jit(solution)/shard_map/pallas_call | solution.py:606
  100.0 0.0 copy-start
  100.0 2.1 %copy.11 = f32[32,1,48,128]{3,2,1,0:T(8,128)} copy(f32[32,1,48,128]{3,2,1,0:T(8,128)} %bitcast.12) | data formatting | bytes 1572864
  102.1 0.0 copy-done
  102.1 0.9 copy.12
Async XLA Ops:
  100.0 2.1 %copy-start = (f32[2,16,48,128]{3,2,1,0:T(8,128)S(1)}, f32[2,16,48,128]{3,2,1,0:T(8,128)}, u32[]{:S(2)}) copy-start(f32[2,16,48,128]{3,2,1,0:T(8,128)} %get-tuple-element.5) | copy-start | bytes 2359300

commit v3 on v2

--- a/solution.py
+++ b/solution.py
@@ -106,7 +106,7 @@
     n, quarters, stages,
     u_hbm, b_hbm, med_hbm, table_hbm, index_hbm, sol_lines, res_lines,
     u_lines, b_lines, med_ref, table_ref, index_ref,
-    u_ref, b_ref, sol_ref, res_ref, ubuf, vbuf, bbuf, mbuf, sh, sl, uh, ul, obuf, gram0, gram, coef, hbt, ebt, lsq, fin, back,
+    u_ref, b_ref, sol_ref, res_ref, ubuf, vbuf, bbuf, mbuf, sh, sl, uh, ul, obuf, gram0, gram, coef, hbt, ebt, lsq, yfirst, fin, back,
     in_sem, in_send, in_recv, z_send, z_recv, x_send, x_recv, red_send, red_recv, out_send, out_recv,
 ):
     me = lax.axis_index("grid")
@@ -464,6 +464,7 @@
                 he = hbt[0:early, :]
                 normal = jnp.concatenate([dot_t(he, he), pads], axis=1)
                 lsq[...] = eliminate(beside(normal, early), early)
+                yfirst[...] = dot(dot_t(lower, he[:, 0:block]), lsq[:, early : 2 * early])
 
             fin[0:block, :] = reduce_sum(gram, j - 1, fin[0:block, :], invert_early)
         else:
@@ -471,39 +472,38 @@
         wa = fin[0:block, 0:pad]
         wa_inv = dot(wa, whole_inv)
         ht = fin[0:block, pad:known]
-        fresh = fin[0:block, known:wide] - dot_t(ht, ht) - dot_t(wa_inv, wa)
+        at = block * (j - 1)
+        ebt[at : at + block, :] = wa_inv
+        outside = fin[0:block, known:wide] - dot_t(wa_inv, wa)
+        if j == STEPS:
+            break
+        fresh = outside - dot_t(ht, ht)
         lt, inv = factor(beside(full(fresh), block), block, block)
         coef[:, 0:pad] = -dot(inv, wa_inv)
         coef[:, pad:known] = -dot(inv, ht)
         coef[:, known:wide] = inv
-        at = block * (j - 1)
         hbt[at : at + block, 0 : known - pad] = ht
         hbt[at : at + block, known - pad : known - pad + block] = dot_t(unit, lt)
-        ebt[at : at + block, :] = wa_inv
 
     width = pad + block * (STEPS + 1)
     kry = block * STEPS
-    he, hl = hbt[0:early, :], hbt[early:kry, :]
+    he, yt0 = hbt[0:early, 0:kry], yfirst[...]
     p = lsq[:, early : 2 * early]
-    rt_early = dot_t(lower, he[:, 0:block])
-    rt_late = dot_t(lower, hl[:, 0:block])
-    cross = dot_t(hl, he)
+    cross = dot_t(ht, he)
     bent = dot(cross, p)
-    schur = dot_t(hl, hl) - dot_t(bent, cross)
-    yt0 = dot(rt_early, p)
-    late_right = rt_late - dot_t(yt0, cross)
+    schur = outside - dot_t(bent, cross)
+    late_right = dot_t(lower, ht[:, 0:block]) - dot_t(yt0, cross)
     both = jnp.concatenate([schur, dot_t(unit, late_right), wide_zero[:, block:]], axis=1)
     y_late = dot_t(unit, eliminate(both, block)[:, block : 2 * block])
-    yt = jnp.concatenate([yt0 - dot(y_late, bent), y_late], axis=1)
+    y_early = yt0 - dot(y_late, bent)
+    yt = jnp.concatenate([y_early, y_late], axis=1)
     back[...] = ba_inv - dot(yt, ebt[...])
-    fin[0:block, :] = -dot(yt, hbt[...])
-    fin[0:block, 0:block] = fin[0:block, 0:block] + lower
-    top = fin[0:block, 0:kry]
-    last = dot(fin[0:block, kry : kry + block], coef[:, 0:width])
     fin[...] = jnp.zeros(fin.shape, jnp.float32)
     fin[0:block, pad : pad + kry] = yt
-    fin[block : 2 * block, 0:width] = last
-    fin[block : 2 * block, pad : pad + kry] = fin[block : 2 * block, pad : pad + kry] + top
+    fin[block : 2 * block, 0:pad] = dot(y_late, wa_inv)
+    fin[block : 2 * block, pad : pad + kry] = -dot(y_early, he)
+    fin[block : 2 * block, pad : pad + block] = fin[block : 2 * block, pad : pad + block] + lower
+    fin[block : 2 * block, pad + kry : width] = -y_late
     high, low = halves(fin[0 : 2 * block, 0:width])
     stacked = jnp.concatenate([high, low], axis=0)
     bh, bl = halves(back[...])
@@ -633,6 +633,7 @@
                 pltpu.VMEM((block * STEPS, LANES), f32),
                 pltpu.VMEM((block * STEPS, pad), f32),
                 pltpu.VMEM((block * (STEPS - 1), LANES), f32),
+                pltpu.VMEM((block, block * (STEPS - 1)), f32),
                 pltpu.VMEM((pad, LANES), f32),
                 pltpu.VMEM((block, pad), f32),
                 sems(5),

time: 103 us -> 102 us (level)
  Pallas kernels: 99.4 us -> 97.8 us
    pallas_call x1, Pallas kernels: 99.4 us -> 97.8 us  [on_device(): pl.pallas_call(functools.partial(kernel, n, quarters, tuple(stages)), out...]
where the time goes in v3:
time: 102 us
  Pallas kernels  97.8 us (96%)
  local copies, waits for them, and re-layouts  3.02 us (3%)
    pallas_call x1, Pallas kernels, on_device(): pl.pallas_call(functools.partial(kernel, n, quarters, tuple(stages)), out...  97.8 us
    unnamed x4, local copies, waits for them, and re-layouts  3.02 us

profile of v3, /device:TPU:0, one launch (start us, length us, event | category | flops | bytes accessed | tf_op | source)
XLA Modules:
  0.0 101.5 jit_solution(15462079084635348683)
XLA Ops:
  0.6 97.8 %shard_map.68 = (f32[2,16,48,128]{3,2,1,0:T(8,128)}, f32[2,16,48,128]{3,2,1,0:T(8,128)}) custom-call(f32[2,24,48,128]{3,2,1,0:T(8,128)} %bitcast.9, f32[2,16,48,128]{3,2,1,0:T(8,128)} %bitcast.10, f32[1,6144]{1,0:T(1,128)} %bitcast.13, f32[8]{0:T(128)} %table_hbm.1, s32[2]{0:T(128)} %index_hbm.1), custom_call_target="tpu_custom_call" | custom-call | tf_op jit(solution)/shard_map/pallas_call | solution.py:606
  98.5 0.0 copy-start
  98.5 2.1 %copy.11 = f32[32,1,48,128]{3,2,1,0:T(8,128)} copy(f32[32,1,48,128]{3,2,1,0:T(8,128)} %bitcast.12) | data formatting | bytes 1572864
  100.6 0.0 copy-done
  100.6 0.9 copy.12
Async XLA Ops:
  98.5 2.1 %copy-start = (f32[2,16,48,128]{3,2,1,0:T(8,128)S(1)}, f32[2,16,48,128]{3,2,1,0:T(8,128)}, u32[]{:S(2)}) copy-start(f32[2,16,48,128]{3,2,1,0:T(8,128)} %get-tuple-element.5) | copy-start | bytes 2359300

commit v4 on v3

--- a/solution.py
+++ b/solution.py
@@ -106,7 +106,7 @@
     n, quarters, stages,
     u_hbm, b_hbm, med_hbm, table_hbm, index_hbm, sol_lines, res_lines,
     u_lines, b_lines, med_ref, table_ref, index_ref,
-    u_ref, b_ref, sol_ref, res_ref, ubuf, vbuf, bbuf, mbuf, sh, sl, uh, ul, obuf, gram0, gram, coef, hbt, ebt, lsq, yfirst, fin, back,
+    u_ref, b_ref, sol_ref, res_ref, ubuf, vbuf, bbuf, mbuf, sh, sl, uh, ul, obuf, gram0, gram, coef, hbt, ebt, lsq, yfirst, aug, fin, back,
     in_sem, in_send, in_recv, z_send, z_recv, x_send, x_recv, red_send, red_recv, out_send, out_recv,
 ):
     me = lax.axis_index("grid")
@@ -357,23 +357,27 @@
     fin[0:k_rows, size:] = jnp.zeros((k_rows, LANES - size), jnp.float32)
     half = LANES // 2
     fin[0:block, half : half + block] = whole[pad:, pad:]
+    after = half + block
+    fin[0:block, after : after + pad] = whole[pad:, 0:pad]
 
     def clear():
         hbt[...] = jnp.zeros(hbt.shape, jnp.float32)
         lsq[...] = jnp.zeros(lsq.shape, jnp.float32)
 
     fin[0:k_rows, :] = reduce_sum(gram0, 0, fin[0:k_rows, :], clear)
-    if pad > k_rows:
-        fin[k_rows:pad, :] = jnp.zeros((pad - k_rows, LANES), jnp.float32)
-    lanes = iota2((pad, LANES), 1)
-    mixed = fin[0:pad, 0:size]
-    linv = factor(beside(jnp.where(lanes < pad, fin[0:pad, :], 0.0), pad), pad, k_rows)[1]
-    whole_inv = lax.dot_general(
-        linv, linv, (((0,), (0,)), ((), ())), precision=highest, preferred_element_type=jnp.float32
-    )
-    ba = dot_t(eye(block), mixed[:, pad:size])
-    ba_inv = dot(ba, whole_inv)
-    remaining = fin[0:block, half : half + block] - dot_t(ba_inv, ba)
+    rows, at_lane = iota2((size, LANES), 0), iota2((size, LANES), 1)
+    aug[...] = jnp.where((at_lane == rows + size) & (rows < k_rows), 1.0, 0.0)
+    aug[0:k_rows, 0:size] = fin[0:k_rows, 0:size]
+    aug[pad:size, 0:pad] = fin[0:block, after : after + pad]
+    aug[pad:size, pad:size] = fin[0:block, half : half + block]
+    x, row = aug[...], rows[:, 0:1]
+    for k in range(0, k_rows, 2):
+        x = pair_step(x, k, row != k, row != k + 1)
+    pivots = jnp.sum(jnp.where(at_lane == rows, x, 0.0), axis=1, keepdims=True)
+    scale = jnp.where(row < k_rows, 1.0 / jnp.where(row < k_rows, pivots, 1.0), 0.0)
+    whole_inv = (x * scale)[0:pad, size : size + pad]
+    ba_inv = -x[pad:size, size : size + pad]
+    remaining = x[pad:size, pad:size]
     wide_zero = jnp.zeros((block, LANES - block), jnp.float32)
     full = lambda m: jnp.concatenate([m, wide_zero], axis=1)
     top_factor, inv = factor(beside(full(remaining), block), block, block)
@@ -634,6 +638,7 @@
                 pltpu.VMEM((block * STEPS, pad), f32),
                 pltpu.VMEM((block * (STEPS - 1), LANES), f32),
                 pltpu.VMEM((block, block * (STEPS - 1)), f32),
+                pltpu.VMEM((pad + block, LANES), f32),
                 pltpu.VMEM((pad, LANES), f32),
                 pltpu.VMEM((block, pad), f32),
                 sems(5),

time: 102 us -> 101 us (level)
  no operation moved by 1% of the time
where the time goes in v4:
time: 101 us
  Pallas kernels  97.6 us (97%)
  local copies, waits for them, and re-layouts  3.02 us (3%)
    pallas_call x1, Pallas kernels, on_device(): pl.pallas_call(functools.partial(kernel, n, quarters, tuple(stages)), out...  97.6 us
    unnamed x4, local copies, waits for them, and re-layouts  3.02 us

profile of v4, /device:TPU:0, one launch (start us, length us, event | category | flops | bytes accessed | tf_op | source)
XLA Modules:
  0.0 101.3 jit_solution(8797919139322474894)
XLA Ops:
  0.6 97.6 %shard_map.68 = (f32[2,16,48,128]{3,2,1,0:T(8,128)}, f32[2,16,48,128]{3,2,1,0:T(8,128)}) custom-call(f32[2,24,48,128]{3,2,1,0:T(8,128)} %bitcast.9, f32[2,16,48,128]{3,2,1,0:T(8,128)} %bitcast.10, f32[1,6144]{1,0:T(1,128)} %bitcast.13, f32[8]{0:T(128)} %table_hbm.1, s32[2]{0:T(128)} %index_hbm.1), custom_call_target="tpu_custom_call" | custom-call | tf_op jit(solution)/shard_map/pallas_call | solution.py:610
  98.2 0.0 copy-start
  98.2 2.1 %copy.11 = f32[32,1,48,128]{3,2,1,0:T(8,128)} copy(f32[32,1,48,128]{3,2,1,0:T(8,128)} %bitcast.12) | data formatting | bytes 1572864
  100.4 0.0 copy-done
  100.4 0.9 copy.12
Async XLA Ops:
  98.2 2.1 %copy-start = (f32[2,16,48,128]{3,2,1,0:T(8,128)S(1)}, f32[2,16,48,128]{3,2,1,0:T(8,128)}, u32[]{:S(2)}) copy-start(f32[2,16,48,128]{3,2,1,0:T(8,128)} %get-tuple-element.5) | copy-start | bytes 2359300
